TPU v7x, 32 devices: a whole 2x2x4 slice. The times are simulated.
32 devices in a mesh: row: 4 (over y, x), col: 4 (over z), depth: 2 (over core).
Axes of the slice: x: 2, y: 2, z: 4, core: 2. Of those that a mesh axis runs over, the one named last changes fastest.
Arguments:
- layers: float32 [2, 4096, 4096], P('depth', 'row', 'col'), may hold values from -3 to 134.2, as said below
Outputs:
- factor: float32 [2, 4096, 512], P(None, 'row', 'depth')
- schur: float32 [4096, 4096], P(('row', 'depth'), 'col')
Inputs may be any that keep to these rules, and one draw needn't show every extreme that they name: Read in matrix order, each layer is symmetric, and the sum over layers is symmetric positive definite with a diagonal of order sqrt(4096).
All inputs are finite; a program needn't handle non-finite values.
Results may differ from a plain program's by a relative error of at most 0.0001.
Values sent between devices are 32-bit elements; how exact they have to be, the bound alone decides.
A program may use at most 192 MiB of HBM per device.

v0:
```python
import jax
import jax.numpy as jnp
from jax import lax
from jax.sharding import PartitionSpec as P

PANEL = 512
PANELS = 2


def broadcast(value, axis, source):
    kept = jnp.where(lax.axis_index(axis) == source, value, 0).astype(value.dtype)
    return lax.psum(kept, axis)


def block_inverse(diagonal, identity_block):
    lower_diag = jnp.linalg.cholesky(diagonal)
    return jax.scipy.linalg.solve_triangular(lower_diag, identity_block, lower=True)


def outer_update(left_rows, right_rows):
    return lax.dot_general(
        left_rows,
        right_rows,
        (((1,), (1,)), ((), ())),
        precision=lax.Precision.HIGHEST,
        preferred_element_type=jnp.float32,
    )


def per_device(layers):
    row_groups = lax.axis_size("row")
    col_groups = lax.axis_size("col")
    depth_groups = lax.axis_size("depth")
    row_index = lax.axis_index("row")
    col_index = lax.axis_index("col")
    depth_index = lax.axis_index("depth")
    layer_part = layers[0]
    rows_local = layer_part.shape[0]
    cols_local = layer_part.shape[1]
    slice_width = PANEL // depth_groups
    quarter_rows = rows_local // depth_groups
    local_blocks = rows_local // PANEL
    row_block = jnp.arange(rows_local, dtype=jnp.int32) // PANEL * row_groups + row_index
    col_block = jnp.arange(cols_local, dtype=jnp.int32) // PANEL * col_groups + col_index
    identity_block = jnp.eye(PANEL, dtype=jnp.float32)
    factor_list = []
    schur = None
    for panel_step in range(PANELS):
        owner_col = panel_step % col_groups
        local_col = panel_step // col_groups
        owner_row = panel_step % row_groups
        local_row = panel_step // row_groups
        column = layer_part[:, local_col * PANEL : (local_col + 1) * PANEL]
        layer_diag = broadcast(
            column[local_row * PANEL : (local_row + 1) * PANEL], "row", owner_row
        )
        diagonal = lax.psum(layer_diag, "depth")
        quarter = lax.psum_scatter(column, "depth", scatter_dimension=0, tiled=True)
        inverse = block_inverse(diagonal, identity_block)
        solved = jnp.dot(quarter, inverse.T, precision=lax.Precision.HIGHEST)
        quarter_block = lax.dynamic_slice_in_dim(
            row_block, depth_index * quarter_rows, quarter_rows, 0
        )
        solved = jnp.where(quarter_block[:, None] >= panel_step, solved, 0.0)
        row_slice = lax.all_to_all(solved, "depth", split_axis=1, concat_axis=0, tiled=True)
        panel_rows = broadcast(row_slice, "col", owner_col)
        factor_list.append(panel_rows)
        update_rows = jnp.where(row_block[:, None] > panel_step, panel_rows, 0.0)
        gathered = lax.all_gather(panel_rows, "row", axis=0, tiled=True)
        grouped = gathered.reshape(
            row_groups // col_groups, col_groups, local_blocks, PANEL, slice_width
        )
        picked = lax.dynamic_index_in_dim(grouped, col_index, 1, keepdims=False)
        column_rows = picked.transpose(1, 0, 2, 3).reshape(cols_local, slice_width)
        update_cols = jnp.where(col_block[:, None] > panel_step, column_rows, 0.0)
        if panel_step + 1 < PANELS:
            layer_part = layer_part - outer_update(update_rows, update_cols)
        else:
            schur = lax.psum_scatter(
                layer_part - outer_update(update_rows, update_cols),
                "depth",
                scatter_dimension=0,
                tiled=True,
            )
    return (jnp.stack(factor_list), schur)


def solution(mesh):
    return jax.shard_map(
        per_device,
        mesh=mesh,
        in_specs=(P("depth", "row", "col"),),
        out_specs=(P(None, "row", "depth"), P(("row", "depth"), "col")),
        check_vma=False,
    )
```

profile of v0, /device:TPU:0, one launch (start us, length us, event | category | flops | bytes accessed | tf_op | source)
XLA Modules:
  0.0 728.1 jit_solution(16254621082217000149)
XLA Ops:
  7.2 5.4 copy.3
  12.6 2.3 slice_select_fusion.1
  14.9 55.3 %all-reduce.8.cloned.1.call-done = f32[512,512]{0,1:T(8,128)} async-done(((f32[512,512]{0,1:T(8,128)}), f32[512,512]{0,1:T(8,128)}) %all-reduce.8.cloned.1.call-update) | async-done | bytes 1048592 | tf_op jit(solution)/shard_map/psum | solution.py:12
  70.3 3.2 slice.112
  73.8 18.3 %all-reduce.10.cloned.1.call-done = f32[512,512]{0,1:T(8,128)} async-done(((f32[512,512]{0,1:T(8,128)}), f32[512,512]{0,1:T(8,128)}) %all-reduce.10.cloned.1.call-update) | async-done | bytes 1048592 | tf_op jit(solution)/shard_map/psum | solution.py:57
  92.0 1.6 copy.4
  93.6 1.4 fusion.16
  95.1 11.7 %cholesky.286 = f32[128,128]{1,0:T(8,128)S(1)} custom-call(f32[128,128]{1,0:T(8,128)S(1)} %cholesky.426), custom_call_target="Cholesky" | custom-call | tf_op jit(solution)/shard_map/jit(cholesky)/cholesky | solution.py:16
  106.8 9.8 %custom-call.27 = f32[1,128,128]{1,2,0:T(8,128)S(1)} custom-call(f32[1,128,128]{2,1,0:T(8,128)S(1)} %get-tuple-element.61), custom_call_target="InvertDiagBlocksLowerTriangular" | custom-call | tf_op jit(solution)/shard_map/jit(cholesky)/cholesky | solution.py:16
  117.4 11.7 %cholesky.305 = f32[128,128]{1,0:T(8,128)S(1)} custom-call(f32[128,128]{1,0:T(8,128)S(1)} %cholesky.430), custom_call_target="Cholesky" | custom-call | tf_op jit(solution)/shard_map/jit(cholesky)/cholesky | solution.py:16
  129.2 10.0 %custom-call.28 = f32[1,128,128]{1,2,0:T(8,128)S(1)} custom-call(f32[1,128,128]{2,1,0:T(8,128)S(1)} %get-tuple-element.58), custom_call_target="InvertDiagBlocksLowerTriangular" | custom-call | tf_op jit(solution)/shard_map/jit(cholesky)/cholesky | solution.py:16
  139.8 11.7 %cholesky.326 = f32[128,128]{1,0:T(8,128)S(1)} custom-call(f32[128,128]{1,0:T(8,128)S(1)} %cholesky.435), custom_call_target="Cholesky" | custom-call | tf_op jit(solution)/shard_map/jit(cholesky)/cholesky | solution.py:16
  151.6 9.8 %custom-call.29 = f32[1,128,128]{1,2,0:T(8,128)S(1)} custom-call(f32[1,128,128]{2,1,0:T(8,128)S(1)} %get-tuple-element.55), custom_call_target="InvertDiagBlocksLowerTriangular" | custom-call | tf_op jit(solution)/shard_map/jit(cholesky)/cholesky | solution.py:16
  162.0 11.7 %cholesky.343 = f32[128,128]{1,0:T(8,128)S(1)} custom-call(f32[128,128]{1,0:T(8,128)S(1)} %convolution_subtract_fusion.13), custom_call_target="Cholesky" | custom-call | tf_op jit(solution)/shard_map/jit(cholesky)/cholesky | solution.py:16
  178.9 8.1 %while.4 = (s32[]{:T(128)}, f32[512,512]{1,0:T(8,128)S(1)}, s32[4,2]{0,1:T(2,128)S(1)}, f32[4,128,128]{2,1,0:T(8,128)S(1)}, s32[]{:T(128)}) while((s32[]{:T(128)}, f32[512,512]{1,0:T(8,128)S(1)}, s32[4,2]{0,1:T(2,128)S(1)}, f32[4,128,128]{2,1,0:T(8,128)S(1)}, s32[]{:T(128)}) %tuple.57), condition=%wide.while_cond, body=%wide.while_body.sunk | while | flops 2 | bytes 131181 | solution.py:17
  179.5 1.4 bitcast_dynamic-update-slice_fusion.4
  181.6 1.4 bitcast_dynamic-update-slice_fusion.4
  183.6 1.4 bitcast_dynamic-update-slice_fusion.4
  185.7 1.4 bitcast_dynamic-update-slice_fusion.4
  187.0 39.3 %custom-call.30 = f32[4,128,128]{1,2,0:T(8,128)S(1)} custom-call(f32[4,128,128]{2,1,0:T(8,128)S(1)} %get-tuple-element.18), custom_call_target="InvertDiagBlocksLowerTriangular" | custom-call | tf_op jit(solution)/shard_map/jit(_solve_triangular)/triangular_solve | solution.py:17
  229.1 1.3 fusion.66
  230.4 3.1 fusion
  233.5 1.3 copy.16
  234.8 5.7 all_to_all.26
  240.6 1.3 copy.7
  242.0 53.2 %all-reduce.12.cloned.1.call-done = f32[1024,256]{1,0:T(8,128)} async-done(((f32[1024,256]{1,0:T(8,128)}), f32[1024,256]{1,0:T(8,128)}) %all-reduce.12.cloned.1.call-update) | async-done | bytes 1048592 | tf_op jit(solution)/shard_map/psum | solution.py:12
  295.3 53.5 %all-gather.3.cloned.1.call-done = f32[4096,256]{1,0:T(8,128)} async-done(((f32[1024,256]{1,0:T(8,128)}), f32[4096,256]{1,0:T(8,128)}) %all-gather.3.cloned.1.call-update) | async-done | bytes 4194320 | tf_op jit(solution)/shard_map/all_gather | solution.py:69
  348.7 1.4 constant_dynamic-slice_fusion.3
  351.2 3.9 convolution_subtract_fusion.1
  355.1 1.9 copy-done.1
  358.2 52.6 %all-reduce.14.cloned.1.call-done = f32[512,512]{0,1:T(8,128)} async-done(((f32[512,512]{0,1:T(8,128)}), f32[512,512]{0,1:T(8,128)}) %all-reduce.14.cloned.1.call-update) | async-done | bytes 1048592 | tf_op jit(solution)/shard_map/psum | solution.py:12
  410.8 3.2 slice.113
  414.2 18.3 %all-reduce.16.cloned.1.call-done = f32[512,512]{0,1:T(8,128)} async-done(((f32[512,512]{0,1:T(8,128)}), f32[512,512]{0,1:T(8,128)}) %all-reduce.16.cloned.1.call-update) | async-done | bytes 1048592 | tf_op jit(solution)/shard_map/psum | solution.py:57
  432.5 1.6 copy.9
  434.1 1.4 fusion.15
  436.5 11.7 %cholesky.358 = f32[128,128]{1,0:T(8,128)S(1)} custom-call(f32[128,128]{1,0:T(8,128)S(1)} %cholesky.439), custom_call_target="Cholesky" | custom-call | tf_op jit(solution)/shard_map/jit(cholesky)/cholesky | solution.py:16
  448.4 9.8 %custom-call.31 = f32[1,128,128]{1,2,0:T(8,128)S(1)} custom-call(f32[1,128,128]{2,1,0:T(8,128)S(1)} %get-tuple-element.51), custom_call_target="InvertDiagBlocksLowerTriangular" | custom-call | tf_op jit(solution)/shard_map/jit(cholesky)/cholesky | solution.py:16
  458.2 1.2 constant_dynamic-update-slice_fusion.3
  459.5 1.3 convolution_subtract_fusion.8
  460.7 11.7 %cholesky.377 = f32[128,128]{1,0:T(8,128)S(1)} custom-call(f32[128,128]{1,0:T(8,128)S(1)} %cholesky.443), custom_call_target="Cholesky" | custom-call | tf_op jit(solution)/shard_map/jit(cholesky)/cholesky | solution.py:16
  472.5 10.0 %custom-call.32 = f32[1,128,128]{1,2,0:T(8,128)S(1)} custom-call(f32[1,128,128]{2,1,0:T(8,128)S(1)} %get-tuple-element.48), custom_call_target="InvertDiagBlocksLowerTriangular" | custom-call | tf_op jit(solution)/shard_map/jit(cholesky)/cholesky | solution.py:16
  482.8 1.3 convolution_subtract_fusion.10
  484.1 11.7 %cholesky.398 = f32[128,128]{1,0:T(8,128)S(1)} custom-call(f32[128,128]{1,0:T(8,128)S(1)} %cholesky.448), custom_call_target="Cholesky" | custom-call | tf_op jit(solution)/shard_map/jit(cholesky)/cholesky | solution.py:16
  495.8 9.8 %custom-call.33 = f32[1,128,128]{1,2,0:T(8,128)S(1)} custom-call(f32[1,128,128]{2,1,0:T(8,128)S(1)} %get-tuple-element.45), custom_call_target="InvertDiagBlocksLowerTriangular" | custom-call | tf_op jit(solution)/shard_map/jit(cholesky)/cholesky | solution.py:16
  507.1 11.7 %cholesky.415 = f32[128,128]{1,0:T(8,128)S(1)} custom-call(f32[128,128]{1,0:T(8,128)S(1)} %convolution_subtract_fusion.12), custom_call_target="Cholesky" | custom-call | tf_op jit(solution)/shard_map/jit(cholesky)/cholesky | solution.py:16
  524.0 1.3 select_select_fusion
  525.3 11.7 %while.5 = (s32[]{:T(128)}, f32[512,512]{1,0:T(8,128)}, s32[4,2]{0,1:T(2,128)S(1)}, f32[4,128,128]{2,1,0:T(8,128)S(1)}, s32[]{:T(128)}) while((s32[]{:T(128)}, f32[512,512]{1,0:T(8,128)}, s32[4,2]{0,1:T(2,128)S(1)}, f32[4,128,128]{2,1,0:T(8,128)S(1)}, s32[]{:T(128)}) %tuple.85), condition=%wide.while_cond.clone, body=%wide.while_body.clone.sunk | while | flops 2 | bytes 131181 | solution.py:17
  526.0 2.3 bitcast_dynamic-update-slice_fusion.5
  529.0 2.3 bitcast_dynamic-update-slice_fusion.5
  531.9 2.3 bitcast_dynamic-update-slice_fusion.5
  534.8 2.2 bitcast_dynamic-update-slice_fusion.5
  537.1 39.3 %custom-call.34 = f32[4,128,128]{1,2,0:T(8,128)S(1)} custom-call(f32[4,128,128]{2,1,0:T(8,128)S(1)} %get-tuple-element.19), custom_call_target="InvertDiagBlocksLowerTriangular" | custom-call | tf_op jit(solution)/shard_map/jit(_solve_triangular)/triangular_solve | solution.py:17
  578.5 1.3 convolution_subtract_fusion.2
  580.2 1.6 convolution_subtract_fusion.6
  582.2 3.1 convolution_select_fusion
  585.3 4.6 all_to_all.27
  590.0 1.3 copy.10
  591.4 53.2 %all-reduce.18.cloned.1.call-done = f32[1024,256]{1,0:T(8,128)} async-done(((f32[1024,256]{1,0:T(8,128)}), f32[1024,256]{1,0:T(8,128)}) %all-reduce.18.cloned.1.call-update) | async-done | bytes 1048592 | tf_op jit(solution)/shard_map/psum | solution.py:12
  644.7 53.5 %all-gather.5.cloned.1.call-done = f32[4096,256]{1,0:T(8,128)} async-done(((f32[1024,256]{1,0:T(8,128)}), f32[4096,256]{1,0:T(8,128)}) %all-gather.5.cloned.1.call-update) | async-done | bytes 4194320 | tf_op jit(solution)/shard_map/all_gather | solution.py:69
  698.1 1.4 constant_dynamic-slice_fusion.2
  700.6 5.5 convolution_subtract_fusion
  706.2 1.5 pad_maximum_fusion
  707.6 10.6 %reduce-scatter.8.cloned.1.call-done = f32[512,1024]{0,1:T(8,128)} async-done(((f32[1024,1024]{0,1:T(8,128)}), f32[512,1024]{0,1:T(8,128)}) %reduce-scatter.8.cloned.1.call-update) | async-done | bytes 2097168 | tf_op jit(solution)/shard_map/reduce_scatter | solution.py:79
  718.2 2.9 copy.12
  (113 shorter events, 25.5 us)
Async XLA Ops:
  7.2 63.1 %all-reduce.8.cloned.1.call-start = ((), (), s32[]{:S(2)}) async-start(), calls=%async_computation.5 | async-start | bytes 2097152 | tf_op jit(solution)/shard_map/psum | solution.py:12
  14.9 77.1 %all-reduce.10.cloned.1.call-start = ((), (), s32[]{:S(2)}) async-start(), calls=%async_computation.6 | async-start | bytes 2097152 | tf_op jit(solution)/shard_map/psum | solution.py:57
  70.3 160.1 %reduce-scatter.4.cloned.1.call-start = ((), (), s32[]{:S(2)}) async-start(), calls=%async_computation.7 | async-start | bytes 3145728 | tf_op jit(solution)/shard_map/reduce_scatter | solution.py:58
  73.5 221.7 %all-reduce.12.cloned.1.call-start = ((), (), s32[]{:S(2)}) async-start(), calls=%async_computation.8 | async-start | bytes 2097152 | tf_op jit(solution)/shard_map/psum | solution.py:12
  226.4 2.1 copy-start.6
  241.9 106.8 %all-gather.3.cloned.1.call-start = ((), (), s32[]{:S(2)}) async-start(), calls=%async_computation.9 | async-start | bytes 5242880 | tf_op jit(solution)/shard_map/all_gather | solution.py:69
  295.2 55.2 %copy-start.3 = (f32[1024,256]{1,0:T(8,128)S(1)}, f32[1024,256]{1,0:T(8,128)}, u32[]{:S(2)}) copy-start(f32[1024,256]{1,0:T(8,128)} %all-reduce.12.cloned.1.call-done) | copy-start | bytes 3145732
  295.2 115.5 %all-reduce.14.cloned.1.call-start = ((), (), s32[]{:S(2)}) async-start(), calls=%async_computation.11 | async-start | bytes 2097152 | tf_op jit(solution)/shard_map/psum | solution.py:12
  348.7 2.5 copy-start
  355.1 1.9 copy-start.1
  358.1 74.4 %all-reduce.16.cloned.1.call-start = ((), (), s32[]{:S(2)}) async-start(), calls=%async_computation.12 | async-start | bytes 2097152 | tf_op jit(solution)/shard_map/psum | solution.py:57
  410.8 171.5 %reduce-scatter.6.cloned.1.call-start = ((), (), s32[]{:S(2)}) async-start(), calls=%async_computation.10 | async-start | bytes 3145728 | tf_op jit(solution)/shard_map/reduce_scatter | solution.py:58
  414.0 230.6 %all-reduce.18.cloned.1.call-start = ((), (), s32[]{:S(2)}) async-start(), calls=%async_computation.13 | async-start | bytes 2097152 | tf_op jit(solution)/shard_map/psum | solution.py:12
  435.5 1.0 copy-start.5
  591.4 106.8 %all-gather.5.cloned.1.call-start = ((), (), s32[]{:S(2)}) async-start(), calls=%async_computation.14 | async-start | bytes 5242880 | tf_op jit(solution)/shard_map/all_gather | solution.py:69
  644.6 55.2 %copy-start.4 = (f32[1024,256]{1,0:T(8,128)S(1)}, f32[1024,256]{1,0:T(8,128)}, u32[]{:S(2)}) copy-start(f32[1024,256]{1,0:T(8,128)} %all-reduce.18.cloned.1.call-done) | copy-start | bytes 3145732
  644.6 73.6 %reduce-scatter.8.cloned.1.call-start = ((), (), s32[]{:S(2)}) async-start(), calls=%async_computation.15 | async-start | bytes 6291456 | tf_op jit(solution)/shard_map/reduce_scatter | solution.py:79
  698.1 2.5 copy-start.2
Sparse Core Ops, SparseCore 0:
  15.0 55.1 all-reduce.7
  72.6 19.4 all-reduce.9
  94.8 10.8 reduce-scatter.3
  242.0 53.0 all-reduce.11
  296.8 51.8 all-gather.2
  358.2 52.4 all-reduce.13
  413.1 19.4 all-reduce.15
  435.3 10.7 reduce-scatter.5
  591.5 53.0 all-reduce.17
  646.3 51.8 all-gather.4
  706.3 11.8 reduce-scatter.7
where the time goes:
time: 738 us; the launch traced here: 728 us
  waiting for transfers between devices  369 us (50%)
  other arithmetic  247 us (33%)
  local copies, waits for them, and re-layouts  49.1 us (7%)
  matrix products  32.6 us (4%)
  between operations  20 us (3%)
  blocking collectives  10.3 us (1%)
    psum x4, waiting for transfers between devices, broadcast(): return lax.psum(kept, axis)  214 us
    another operation x29, other arithmetic, block_inverse(): lower_diag = jnp.linalg.cholesky(diagonal)  158 us
    all_gather x2, waiting for transfers between devices, per_device(): gathered = lax.all_gather(panel_rows, 'row', axis=0, tiled=True)  107 us
    another operation x5, other arithmetic, block_inverse(): jax.scipy.linalg.solve_triangular(lower_diag, identity_block, lower=True)  80.1 us
    psum x2, waiting for transfers between devices, per_device(): diagonal = lax.psum(layer_diag, 'depth')  36.6 us
    another operation x27, local copies, waits for them, and re-layouts, block_inverse(): jax.scipy.linalg.solve_triangular(lower_diag, identity_block, lower=True)  19.7 us
  transfers between devices with their start and end apart: 11, of which 9 were waited for; matrix products, arithmetic and copies ran while one was open for 40% of the time, Pallas kernels for 0%

commit v1 on v0

--- a/solution.py
+++ b/solution.py
@@ -54,7 +54,8 @@
         layer_diag = broadcast(
             column[local_row * PANEL : (local_row + 1) * PANEL], "row", owner_row
         )
-        diagonal = lax.psum(layer_diag, "depth")
+        parts = lax.all_gather(layer_diag, "depth")
+        diagonal = jnp.sum(parts, axis=0)
         quarter = lax.psum_scatter(column, "depth", scatter_dimension=0, tiled=True)
         inverse = block_inverse(diagonal, identity_block)
         solved = jnp.dot(quarter, inverse.T, precision=lax.Precision.HIGHEST)

time: 738 us -> 714 us (0.967)
  waiting for transfers between devices: 369 us -> 351 us
  local copies, waits for them, and re-layouts: 49.1 us -> 38.7 us
    psum x2 -> x0, waiting for transfers between devices: 36.6 us -> none  [per_device(): diagonal = lax.psum(layer_diag, 'depth')]
    all_gather x0 -> x2, waiting for transfers between devices: none -> 17.4 us  [per_device(): parts = lax.all_gather(layer_diag, 'depth')]
  transfers between devices with their start and end apart: 11 -> 11, of which waited for: 9 -> 9; matrix products, arithmetic and copies ran while one was open for 40% -> 42% of each run, Pallas kernels for 0% -> 0%
where the time goes in v1:
time: 714 us; the launch traced here: 704 us
  waiting for transfers between devices  351 us (49%)
  other arithmetic  249 us (35%)
  local copies, waits for them, and re-layouts  38.7 us (5%)
  matrix products  35 us (5%)
  between operations  19.8 us (3%)
  blocking collectives  9.15 us (1%)
    psum x4, waiting for transfers between devices, broadcast(): return lax.psum(kept, axis)  216 us
    another operation x29, other arithmetic, block_inverse(): lower_diag = jnp.linalg.cholesky(diagonal)  158 us
    all_gather x2, waiting for transfers between devices, per_device(): gathered = lax.all_gather(panel_rows, 'row', axis=0, tiled=True)  107 us
    another operation x5, other arithmetic, block_inverse(): jax.scipy.linalg.solve_triangular(lower_diag, identity_block, lower=True)  79.9 us
    another operation x27, local copies, waits for them, and re-layouts, block_inverse(): jax.scipy.linalg.solve_triangular(lower_diag, identity_block, lower=True)  19.2 us
    all_gather x2, waiting for transfers between devices, per_device(): parts = lax.all_gather(layer_diag, 'depth')  17.4 us
  transfers between devices with their start and end apart: 11, of which 9 were waited for; matrix products, arithmetic and copies ran while one was open for 42% of the time, Pallas kernels for 0%

profile of v1, /device:TPU:0, one launch (start us, length us, event | category | flops | bytes accessed | tf_op | source)
XLA Modules:
  0.0 704.3 jit_solution(365314277607581835)
XLA Ops:
  7.2 2.3 fusion.1
  9.6 57.3 %all-reduce.6.cloned.1.call-done = f32[1,512,512]{2,1,0:T(8,128)} async-done(((f32[1,512,512]{2,1,0:T(8,128)}), f32[1,512,512]{2,1,0:T(8,128)}) %all-reduce.6.cloned.1.call-update) | async-done | bytes 1048592 | tf_op jit(solution)/shard_map/psum | solution.py:12
  66.9 3.1 slice.112
  70.3 8.7 %all-gather.5.cloned.1.call-done = f32[2,512,512]{2,1,0:T(8,128)} async-done(((f32[1,512,512]{2,1,0:T(8,128)}), f32[2,512,512]{2,1,0:T(8,128)}) %all-gather.5.cloned.1.call-update) | async-done | bytes 2097168 | tf_op jit(solution)/shard_map/all_gather | solution.py:57
  79.0 1.9 reduce_sum.18
  82.4 11.7 %cholesky.286 = f32[128,128]{1,0:T(8,128)S(1)} custom-call(f32[128,128]{1,0:T(8,128)S(1)} %cholesky.426), custom_call_target="Cholesky" | custom-call | tf_op jit(solution)/shard_map/jit(cholesky)/cholesky | solution.py:16
  94.2 9.8 %custom-call.27 = f32[1,128,128]{1,2,0:T(8,128)S(1)} custom-call(f32[1,128,128]{2,1,0:T(8,128)S(1)} %get-tuple-element.59), custom_call_target="InvertDiagBlocksLowerTriangular" | custom-call | tf_op jit(solution)/shard_map/jit(cholesky)/cholesky | solution.py:16
  104.1 1.2 constant_dynamic-update-slice_fusion.5
  105.4 1.3 convolution_subtract_fusion.9
  106.6 11.7 %cholesky.305 = f32[128,128]{1,0:T(8,128)S(1)} custom-call(f32[128,128]{1,0:T(8,128)S(1)} %cholesky.430), custom_call_target="Cholesky" | custom-call | tf_op jit(solution)/shard_map/jit(cholesky)/cholesky | solution.py:16
  118.4 10.2 %custom-call.28 = f32[1,128,128]{1,2,0:T(8,128)S(1)} custom-call(f32[1,128,128]{2,1,0:T(8,128)S(1)} %get-tuple-element.56), custom_call_target="InvertDiagBlocksLowerTriangular" | custom-call | tf_op jit(solution)/shard_map/jit(cholesky)/cholesky | solution.py:16
  128.9 1.3 convolution_subtract_fusion.11
  130.2 11.7 %cholesky.326 = f32[128,128]{1,0:T(8,128)S(1)} custom-call(f32[128,128]{1,0:T(8,128)S(1)} %cholesky.435), custom_call_target="Cholesky" | custom-call | tf_op jit(solution)/shard_map/jit(cholesky)/cholesky | solution.py:16
  142.0 9.8 %custom-call.29 = f32[1,128,128]{1,2,0:T(8,128)S(1)} custom-call(f32[1,128,128]{2,1,0:T(8,128)S(1)} %get-tuple-element.53), custom_call_target="InvertDiagBlocksLowerTriangular" | custom-call | tf_op jit(solution)/shard_map/jit(cholesky)/cholesky | solution.py:16
  152.0 1.2 convolution_subtract_fusion.13
  153.2 11.9 %cholesky.343 = f32[128,128]{1,0:T(8,128)S(1)} custom-call(f32[128,128]{1,0:T(8,128)S(1)} %convolution_subtract_fusion.13), custom_call_target="Cholesky" | custom-call | tf_op jit(solution)/shard_map/jit(cholesky)/cholesky | solution.py:16
  169.7 7.6 %while.4 = (s32[]{:T(128)}, f32[512,512]{1,0:T(8,128)S(1)}, s32[4,2]{0,1:T(2,128)S(1)}, f32[4,128,128]{2,1,0:T(8,128)S(1)}, s32[]{:T(128)}) while((s32[]{:T(128)}, f32[512,512]{1,0:T(8,128)S(1)}, s32[4,2]{0,1:T(2,128)S(1)}, f32[4,128,128]{2,1,0:T(8,128)S(1)}, s32[]{:T(128)}) %tuple.56), condition=%wide.while_cond, body=%wide.while_body.sunk | while | flops 2 | bytes 131181 | solution.py:17
  170.3 1.3 bitcast_dynamic-update-slice_fusion.4
  172.2 1.3 bitcast_dynamic-update-slice_fusion.4
  174.1 1.3 bitcast_dynamic-update-slice_fusion.4
  176.0 1.3 bitcast_dynamic-update-slice_fusion.4
  177.3 39.3 %custom-call.30 = f32[4,128,128]{1,2,0:T(8,128)S(1)} custom-call(f32[4,128,128]{2,1,0:T(8,128)S(1)} %get-tuple-element.18), custom_call_target="InvertDiagBlocksLowerTriangular" | custom-call | tf_op jit(solution)/shard_map/jit(_solve_triangular)/triangular_solve | solution.py:17
  219.8 3.1 convolution_select_fusion.1
  222.9 4.6 all_to_all.26
  227.6 1.3 copy.10
  229.0 53.2 %all-reduce.8.cloned.1.call-done = f32[1024,256]{1,0:T(8,128)} async-done(((f32[1024,256]{1,0:T(8,128)}), f32[1024,256]{1,0:T(8,128)}) %all-reduce.8.cloned.1.call-update) | async-done | bytes 1048592 | tf_op jit(solution)/shard_map/psum | solution.py:12
  282.2 53.5 %all-gather.7.cloned.1.call-done = f32[4096,256]{1,0:T(8,128)} async-done(((f32[1024,256]{1,0:T(8,128)}), f32[4096,256]{1,0:T(8,128)}) %all-gather.7.cloned.1.call-update) | async-done | bytes 4194320 | tf_op jit(solution)/shard_map/all_gather | solution.py:70
  335.7 1.4 constant_dynamic-slice_fusion.3
  338.2 3.8 convolution_subtract_fusion.1
  342.0 1.9 copy-done
  345.1 52.6 %all-reduce.10.cloned.1.call-done = f32[1,512,512]{2,1,0:T(8,128)} async-done(((f32[1,512,512]{2,1,0:T(8,128)}), f32[1,512,512]{2,1,0:T(8,128)}) %all-reduce.10.cloned.1.call-update) | async-done | bytes 1048592 | tf_op jit(solution)/shard_map/psum | solution.py:12
  397.7 3.1 slice.113
  401.1 8.7 %all-gather.9.cloned.1.call-done = f32[2,512,512]{2,1,0:T(8,128)} async-done(((f32[1,512,512]{2,1,0:T(8,128)}), f32[2,512,512]{2,1,0:T(8,128)}) %all-gather.9.cloned.1.call-update) | async-done | bytes 2097168 | tf_op jit(solution)/shard_map/all_gather | solution.py:57
  409.8 1.9 reduce_sum.19
  411.7 1.3 copy.11
  413.0 1.4 fusion.16
  415.4 11.7 %cholesky.358 = f32[128,128]{1,0:T(8,128)S(1)} custom-call(f32[128,128]{1,0:T(8,128)S(1)} %cholesky.439), custom_call_target="Cholesky" | custom-call | tf_op jit(solution)/shard_map/jit(cholesky)/cholesky | solution.py:16
  427.3 9.8 %custom-call.31 = f32[1,128,128]{1,2,0:T(8,128)S(1)} custom-call(f32[1,128,128]{2,1,0:T(8,128)S(1)} %get-tuple-element.49), custom_call_target="InvertDiagBlocksLowerTriangular" | custom-call | tf_op jit(solution)/shard_map/jit(cholesky)/cholesky | solution.py:16
  437.1 1.2 constant_dynamic-update-slice_fusion.3
  438.4 1.3 convolution_subtract_fusion.8
  439.7 11.7 %cholesky.377 = f32[128,128]{1,0:T(8,128)S(1)} custom-call(f32[128,128]{1,0:T(8,128)S(1)} %cholesky.443), custom_call_target="Cholesky" | custom-call | tf_op jit(solution)/shard_map/jit(cholesky)/cholesky | solution.py:16
  451.4 10.2 %custom-call.32 = f32[1,128,128]{1,2,0:T(8,128)S(1)} custom-call(f32[1,128,128]{2,1,0:T(8,128)S(1)} %get-tuple-element.46), custom_call_target="InvertDiagBlocksLowerTriangular" | custom-call | tf_op jit(solution)/shard_map/jit(cholesky)/cholesky | solution.py:16
  461.9 1.3 convolution_subtract_fusion.10
  463.2 11.7 %cholesky.398 = f32[128,128]{1,0:T(8,128)S(1)} custom-call(f32[128,128]{1,0:T(8,128)S(1)} %cholesky.448), custom_call_target="Cholesky" | custom-call | tf_op jit(solution)/shard_map/jit(cholesky)/cholesky | solution.py:16
  474.9 9.8 %custom-call.33 = f32[1,128,128]{1,2,0:T(8,128)S(1)} custom-call(f32[1,128,128]{2,1,0:T(8,128)S(1)} %get-tuple-element.43), custom_call_target="InvertDiagBlocksLowerTriangular" | custom-call | tf_op jit(solution)/shard_map/jit(cholesky)/cholesky | solution.py:16
  485.0 1.2 convolution_subtract_fusion.12
  486.2 11.9 %cholesky.415 = f32[128,128]{1,0:T(8,128)S(1)} custom-call(f32[128,128]{1,0:T(8,128)S(1)} %convolution_subtract_fusion.12), custom_call_target="Cholesky" | custom-call | tf_op jit(solution)/shard_map/jit(cholesky)/cholesky | solution.py:16
  504.5 11.8 %while.5 = (s32[]{:T(128)}, f32[512,512]{1,0:T(8,128)}, s32[4,2]{0,1:T(2,128)S(1)}, f32[4,128,128]{2,1,0:T(8,128)S(1)}, s32[]{:T(128)}) while((s32[]{:T(128)}, f32[512,512]{1,0:T(8,128)}, s32[4,2]{0,1:T(2,128)S(1)}, f32[4,128,128]{2,1,0:T(8,128)S(1)}, s32[]{:T(128)}) %tuple.84), condition=%wide.while_cond.clone, body=%wide.while_body.clone.sunk | while | flops 2 | bytes 131181 | solution.py:17
  505.2 2.3 bitcast_dynamic-update-slice_fusion.5
  508.1 2.3 bitcast_dynamic-update-slice_fusion.5
  511.1 2.3 bitcast_dynamic-update-slice_fusion.5
  514.0 2.2 bitcast_dynamic-update-slice_fusion.5
  516.3 39.3 %custom-call.34 = f32[4,128,128]{1,2,0:T(8,128)S(1)} custom-call(f32[4,128,128]{2,1,0:T(8,128)S(1)} %get-tuple-element.19), custom_call_target="InvertDiagBlocksLowerTriangular" | custom-call | tf_op jit(solution)/shard_map/jit(_solve_triangular)/triangular_solve | solution.py:17
  557.6 1.3 convolution_subtract_fusion.2
  559.4 1.6 convolution_subtract_fusion.6
  561.4 3.1 convolution_select_fusion
  564.9 4.6 all_to_all.27
  569.5 1.3 copy.14
  570.9 53.2 %all-reduce.12.cloned.1.call-done = f32[1024,256]{1,0:T(8,128)} async-done(((f32[1024,256]{1,0:T(8,128)}), f32[1024,256]{1,0:T(8,128)}) %all-reduce.12.cloned.1.call-update) | async-done | bytes 1048592 | tf_op jit(solution)/shard_map/psum | solution.py:12
  624.2 53.5 %all-gather.11.cloned.1.call-done = f32[4096,256]{1,0:T(8,128)} async-done(((f32[1024,256]{1,0:T(8,128)}), f32[4096,256]{1,0:T(8,128)}) %all-gather.11.cloned.1.call-update) | async-done | bytes 4194320 | tf_op jit(solution)/shard_map/all_gather | solution.py:70
  677.7 1.4 constant_dynamic-slice_fusion.2
  680.2 5.2 convolution_subtract_fusion
  685.4 1.5 pad_maximum_fusion
  686.9 10.7 %reduce-scatter.8.cloned.1.call-done = f32[512,1024]{1,0:T(8,128)} async-done(((f32[1024,1024]{1,0:T(8,128)}), f32[512,1024]{1,0:T(8,128)}) %reduce-scatter.8.cloned.1.call-update) | async-done | bytes 2097168 | tf_op jit(solution)/shard_map/reduce_scatter | solution.py:80
  (113 shorter events, 25.6 us)
Async XLA Ops:
  7.2 59.7 %all-reduce.6.cloned.1.call-start = ((), (), s32[]{:S(2)}) async-start(), calls=%async_computation.5 | async-start | bytes 2097152 | tf_op jit(solution)/shard_map/psum | solution.py:12
  9.5 69.5 %all-gather.5.cloned.1.call-start = ((), (), s32[]{:S(2)}) async-start(), calls=%async_computation.6 | async-start | bytes 3145728 | tf_op jit(solution)/shard_map/all_gather | solution.py:57
  66.9 153.0 %reduce-scatter.4.cloned.1.call-start = ((), (), s32[]{:S(2)}) async-start(), calls=%async_computation.7 | async-start | bytes 3145728 | tf_op jit(solution)/shard_map/reduce_scatter | solution.py:59
  70.0 212.1 %all-reduce.8.cloned.1.call-start = ((), (), s32[]{:S(2)}) async-start(), calls=%async_computation.8 | async-start | bytes 2097152 | tf_op jit(solution)/shard_map/psum | solution.py:12
  81.4 1.0 copy-start.5
  228.9 106.8 %all-gather.7.cloned.1.call-start = ((), (), s32[]{:S(2)}) async-start(), calls=%async_computation.9 | async-start | bytes 5242880 | tf_op jit(solution)/shard_map/all_gather | solution.py:70
  282.1 55.2 %copy-start.3 = (f32[1024,256]{1,0:T(8,128)S(1)}, f32[1024,256]{1,0:T(8,128)}, u32[]{:S(2)}) copy-start(f32[1024,256]{1,0:T(8,128)} %all-reduce.8.cloned.1.call-done) | copy-start | bytes 3145732
  282.2 115.5 %all-reduce.10.cloned.1.call-start = ((), (), s32[]{:S(2)}) async-start(), calls=%async_computation.11 | async-start | bytes 2097152 | tf_op jit(solution)/shard_map/psum | solution.py:12
  335.7 2.5 copy-start.2
  342.0 1.9 copy-start
  345.0 64.8 %all-gather.9.cloned.1.call-start = ((), (), s32[]{:S(2)}) async-start(), calls=%async_computation.12 | async-start | bytes 3145728 | tf_op jit(solution)/shard_map/all_gather | solution.py:57
  397.7 163.7 %reduce-scatter.6.cloned.1.call-start = ((), (), s32[]{:S(2)}) async-start(), calls=%async_computation.10 | async-start | bytes 3145728 | tf_op jit(solution)/shard_map/reduce_scatter | solution.py:59
  400.8 223.2 %all-reduce.12.cloned.1.call-start = ((), (), s32[]{:S(2)}) async-start(), calls=%async_computation.13 | async-start | bytes 2097152 | tf_op jit(solution)/shard_map/psum | solution.py:12
  414.5 1.0 copy-start.6
  570.9 106.8 %all-gather.11.cloned.1.call-start = ((), (), s32[]{:S(2)}) async-start(), calls=%async_computation.14 | async-start | bytes 5242880 | tf_op jit(solution)/shard_map/all_gather | solution.py:70
  624.1 55.2 %copy-start.4 = (f32[1024,256]{1,0:T(8,128)S(1)}, f32[1024,256]{1,0:T(8,128)}, u32[]{:S(2)}) copy-start(f32[1024,256]{1,0:T(8,128)} %all-reduce.12.cloned.1.call-done) | copy-start | bytes 3145732
  624.1 73.5 %reduce-scatter.8.cloned.1.call-start = ((), (), s32[]{:S(2)}) async-start(), calls=%async_computation.15 | async-start | bytes 6291456 | tf_op jit(solution)/shard_map/reduce_scatter | solution.py:80
  677.6 2.5 copy-start.1
Sparse Core Ops, SparseCore 0:
  11.6 55.1 all-reduce.5
  68.4 10.5 all-gather.4
  81.8 10.9 reduce-scatter.3
  229.0 53.0 all-reduce.7
  283.8 51.8 all-gather.6
  345.2 52.4 all-reduce.9
  399.2 10.5 all-gather.8
  412.6 10.9 reduce-scatter.5
  571.0 53.0 all-reduce.11
  625.8 51.8 all-gather.10
  685.5 12.0 reduce-scatter.7
